TPU v7x, 128 devices: a whole 4x4x4 slice. The times are simulated.
128 devices in a mesh: dp: 4 (over z), expert: 16 (over y, x_hi, core), tensor: 2 (over x_lo).
Axes of the slice: x: 4 (x_hi: 2, x_lo: 2; x = x_hi * 2 + x_lo), y: 4, z: 4, core: 2. Of those that a mesh axis runs over, the one named last changes fastest.
Arguments:
- hidden: bfloat16 [8192, 6144], P(('dp', 'expert'), 'tensor'), may hold values from -6 to 6
- expert_ids: int32 [8192, 8], P(('dp', 'expert')), may hold values from 0 to 383, as said below
- gate_fixed: int32 [8192, 8], P(('dp', 'expert')), may hold values from 4096 to 65535
- slot_expert: int32 [64], replicated, may hold values from 0 to 383, as said below
- expert_in: bfloat16 [64, 6144, 2, 1024], P(('dp', 'expert'), 'tensor'), may hold values from -1 to 1, as said below
- expert_out: bfloat16 [64, 1024, 6144], P(('dp', 'expert'), None, 'tensor'), may hold values from -1 to 1, as said below
- shared_in: bfloat16 [6144, 2, 1024], P('tensor', None, 'dp'), may hold values from -0.078125 to 0.078125
- shared_out: bfloat16 [1024, 6144], P('dp', 'tensor'), may hold values from -0.1875 to 0.1875
Outputs:
- mixed: bfloat16 [8192, 6144], P(('dp', 'expert'), 'tensor')
Inputs may be any that keep to these rules, and one draw needn't show every extreme that they name: `expert_ids`: each row names 8 different experts. `slot_expert`: 56 different experts fill the 64 slots; 8 of them hold two slots each, the others one. `expert_in`: slots that hold the same expert hold the same weights. `expert_out`: slots that hold the same expert hold the same weights.
All inputs are finite; a program needn't handle non-finite values.
Results may differ from a plain program's by a relative error of at most 0.006.
Values may be sent and summed in bfloat16 or wider, within the bound.
No kernel may reach another device: no remote copies, remote signals or barrier semaphores. Data moves between devices by JAX's collectives and lax.ppermute only.
A program may use at most 192 MiB of HBM per device.

v0:
```python
import jax
import jax.numpy as jnp
from jax import lax
from jax.sharding import PartitionSpec as P

EXPERTS = 384
CAP = 4
gate_scale = 1.0 / 65536.0


def in_blocks(array, dim, devices):
    before, after = (array.shape[:dim], array.shape[dim + 1 :])
    return jnp.moveaxis(array.reshape(*before, devices, -1, *after), dim, 0)


def summed_on_arrival(array, axis, dim):
    parts = in_blocks(array, dim, lax.axis_size(axis))
    arrived = lax.all_to_all(parts, axis, split_axis=0, concat_axis=0, tiled=True)
    return arrived.astype(jnp.float32).sum(axis=0)


def swiglu(pre):
    return (jax.nn.silu(pre[:, 0, :]) * pre[:, 1, :]).astype(jnp.bfloat16)


def route_plan(chosen, row_rank, slot_expert):
    slot_count = slot_expert.shape[0]
    slot_iota = jnp.arange(slot_count, dtype=jnp.int32)[:, None]
    owns = slot_expert[:, None] == jnp.arange(chosen.shape[2], dtype=jnp.int32)[None, :]
    home = jnp.min(jnp.where(owns, slot_iota, slot_count), axis=0)
    spare = jnp.min(jnp.where(owns & (slot_iota != home[None, :]), slot_iota, slot_count), axis=0)
    home_of = jnp.sum(jnp.where(chosen, home[None, None, :], 0), axis=2)
    spare_of = jnp.sum(jnp.where(chosen, spare[None, None, :], 0), axis=2)
    first = row_rank < CAP
    spill = (row_rank >= CAP) & (row_rank < 2 * CAP) & (spare_of < slot_count)
    target = jnp.where(first, home_of, jnp.where(spill, spare_of, slot_count))
    slot_row = jnp.where(first, row_rank, row_rank - CAP)
    return (target, slot_row)


def dispatch_rows(send_rows):
    return lax.all_to_all(send_rows, ("dp", "expert"), split_axis=0, concat_axis=0, tiled=True)


def return_rows(answers):
    return lax.all_to_all(answers, ("dp", "expert"), split_axis=0, concat_axis=0, tiled=True)


def shards(
    hidden, expert_ids, gate_fixed, slot_expert, expert_in, expert_out, shared_in, shared_out
):
    tok_rows, half_width = hidden.shape
    topk_count = expert_ids.shape[1]
    slot_count = slot_expert.shape[0]
    experts_iota = jnp.arange(EXPERTS, dtype=jnp.int32)
    chosen = expert_ids[:, :, None] == experts_iota[None, None, :]
    picked = jnp.any(chosen, axis=1).astype(jnp.bfloat16)
    token_iota = jnp.arange(tok_rows, dtype=jnp.int32)
    earlier = (token_iota[:, None] > token_iota[None, :]).astype(jnp.bfloat16)
    before = jnp.dot(earlier, picked, preferred_element_type=jnp.float32)
    row_rank = jnp.sum(jnp.where(chosen, before[:, None, :], 0.0), axis=2).astype(jnp.int32)
    target, slot_row = route_plan(chosen, row_rank, slot_expert)
    flat_row = jnp.where(target < slot_count, target * CAP + slot_row, -1)
    row_iota = jnp.arange(slot_count * CAP, dtype=jnp.int32)
    owner = jnp.repeat(token_iota, topk_count)
    match_rows = flat_row.reshape(-1)[:, None] == row_iota[None, :]
    source_token = jnp.max(jnp.where(match_rows, owner[:, None], -1), axis=0)
    fetched_rows = jnp.take(hidden, jnp.maximum(source_token, 0), axis=0)
    send_rows = jnp.where(source_token[:, None] >= 0, fetched_rows, jnp.zeros((), jnp.bfloat16))
    piece = lax.all_gather(hidden, "dp", axis=0, tiled=True)
    partial_value = jnp.dot(
        piece, shared_in.reshape(half_width, -1), preferred_element_type=jnp.float32
    )
    shared_partial = partial_value.reshape(piece.shape[0], 2, -1)
    arrived = dispatch_rows(send_rows.reshape(slot_count, CAP, half_width))
    rows = arrived.reshape(-1, half_width)
    partial_value = jnp.dot(
        rows, expert_in[0].reshape(half_width, -1), preferred_element_type=jnp.float32
    )
    routed_partial = partial_value.reshape(rows.shape[0], 2, -1)
    shared_half, routed_half = (
        lax.psum_scatter(shared_partial, "tensor", scatter_dimension=2, tiled=True),
        lax.psum_scatter(routed_partial, "tensor", scatter_dimension=2, tiled=True),
    )
    shared_act, routed_act = (
        lax.all_gather(swiglu(shared_half), "tensor", axis=1, tiled=True),
        lax.all_gather(swiglu(routed_half), "tensor", axis=1, tiled=True),
    )
    shared_part = summed_on_arrival(
        jnp.dot(shared_act, shared_out, preferred_element_type=jnp.float32).astype(jnp.bfloat16),
        "dp",
        0,
    )
    answers = jnp.dot(routed_act, expert_out[0], preferred_element_type=jnp.float32).astype(
        jnp.bfloat16
    )
    returned = return_rows(answers.reshape(slot_count, CAP, half_width))
    returned = returned.reshape(-1, half_width)
    gates = gate_fixed.astype(jnp.float32) * gate_scale
    routed = jnp.zeros((tok_rows, half_width), jnp.float32)
    for column in range(topk_count):
        index = flat_row[:, column]
        answer_rows = jnp.take(returned, jnp.maximum(index, 0), axis=0).astype(jnp.float32)
        routed = routed + jnp.where(
            index[:, None] >= 0, gates[:, column : column + 1] * answer_rows, 0.0
        )
    return (shared_part + routed).astype(jnp.bfloat16)


def solution(mesh):
    in_specs = (
        P(("dp", "expert"), "tensor"),
        P(("dp", "expert"), None),
        P(("dp", "expert"), None),
        P(),
        P(("dp", "expert"), "tensor", None, None),
        P(("dp", "expert"), None, "tensor"),
        P("tensor", None, "dp"),
        P("dp", "tensor"),
    )
    out_specs = P(("dp", "expert"), "tensor")
    return jax.shard_map(shards, mesh=mesh, in_specs=in_specs, out_specs=out_specs, check_vma=False)
```

profile of v0, /device:TPU:1, one launch (start us, length us, event | category | flops | bytes accessed | tf_op | source)
XLA Modules:
  0.0 226.1 jit_solution(16265131079100112803)
XLA Ops:
  10.4 4.8 %select_reduce_fusion = (s32[128,8]{1,0:T(8,128)S(1)}, s32[128,8]{1,0:T(8,128)S(1)}) fusion(s32[384]{0:T(512)S(1)} %select_reduce_fusion.4, s32[128,8]{1,0:T(8,128)S(1)} %copy.22, s32[384]{0:T(512)S(1)} %select_reduce_fusion.5), kind=kLoop, calls=%fused_computation.18 | loop fusion | flops 1964032 | bytes 15360 | tf_op jit(solution)/shard_map/reduce_sum | solution.py:33
  17.3 2.7 %gather_fusion = bf16[256,3072]{1,0:T(8,128)(2,1)} fusion(bf16[128,3072]{1,0:T(8,128)(2,1)S(1)} %copy-done.1, s32[1024]{0:T(1024)S(1)} %pad_clamp_fusion.8), kind=kCustom, calls=%fused_computation.8 | custom fusion | bytes 3146752 | tf_op jit(solution)/shard_map/jit(_take)/gather | solution.py:68
  20.0 2.9 %gather.10 = bf16[64,4,3072]{2,1,0:T(4,128)(2,1)S(1)} reshape(bf16[256,3072]{1,0:T(8,128)(2,1)} %gather_fusion) | data formatting | bytes 3145728 | tf_op jit(solution)/shard_map/jit(_take)/gather | solution.py:68
  23.0 2.4 %select_select_fusion = bf16[64,4,3072]{2,1,0:T(4,128)(2,1)} fusion(bf16[64,4,3072]{2,1,0:T(4,128)(2,1)S(1)} %gather.10, pred[64,4]{1,0:T(8,128)(4,1)S(1)} %le.24, pred[64,4]{1,0:T(8,128)(4,1)S(1)} %ge.64), kind=kLoop, calls=%fused_computation.17 | loop fusion | flops 1572864 | bytes 3146240 | tf_op jit(solution)/shard_map/jit(_where)/select_n | solution.py:69
  25.4 12.5 %all-to-all-start.1 = ((bf16[64,4,3072]{2,1,0:T(4,128)(2,1)}), bf16[64,4,3072]{2,1,0:T(4,128)(2,1)S(1)}, u32[]{:S(2)}, u32[]{:S(2)}) async-start(bf16[64,4,3072]{2,1,0:T(4,128)(2,1)} %select_select_fusion), calls=%async_computation.2 | async-start | bytes 3145728 | tf_op jit(solution)/shard_map/all_to_all | solution.py:42
  38.1 13.1 %copy.25 = bf16[384,8,2,1024]{3,1,2,0:T(8,128)(2,1)} copy(bf16[384,8,2,1024]{3,2,1,0:T(2,128)(2,1)} %bitcast.65) | data formatting | bytes 25165824
  51.2 16.6 %copy.23 = bf16[2048,3072]{1,0:T(8,128)(2,1)} copy(bf16[2048,3072]{0,1:T(8,128)(2,1)} %bitcast.63) | data formatting | bytes 25165824 | tf_op jit(solution)/shard_map/dot_general | solution.py:77
  69.2 9.9 %fusion.18 = f32[256,2,1024]{2,0,1:T(8,128)} fusion(bf16[256,3072,1]{1,0,2:T(8,128)(2,1)} %reshape.218, bf16[2,1024,3072]{2,1,0:T(8,128)(2,1)} %bitcast.66), kind=kOutput, calls=%fused_computation.101 | convolution fusion | flops 3221225472 | bytes 16252928 | tf_op jit(solution)/shard_map/dot_general | solution.py:77
  79.2 4.1 %copy.24 = bf16[384,8,2,256]{3,1,2,0:T(8,128)(2,1)} copy(bf16[384,8,2,256]{3,2,1,0:T(2,128)(2,1)} %bitcast.68) | data formatting | bytes 6291456
  83.3 4.6 %copy.21 = bf16[512,3072]{1,0:T(8,128)(2,1)} copy(bf16[512,3072]{0,1:T(8,128)(2,1)} %bitcast.67) | data formatting | bytes 6291456 | tf_op jit(solution)/shard_map/dot_general | solution.py:71
  87.9 6.4 %fusion.5 = f32[512,2,256]{2,0,1:T(8,128)} fusion(bf16[2,256,3072]{2,1,0:T(8,128)(2,1)} %bitcast.69, bf16[512,3072]{1,0:T(8,128)(2,1)} %all-gather.2.cloned.1.call-done), kind=kOutput, calls=%fused_computation.14 | convolution fusion | flops 1610612736 | bytes 7340032 | tf_op jit(solution)/shard_map/dot_general | solution.py:71
  94.4 20.0 %reduce-scatter.5.cloned.1.call-done = f32[256,2,512]{2,0,1:T(8,128)} async-done(((f32[256,2,1024]{2,0,1:T(8,128)}), f32[256,2,512]{2,0,1:T(8,128)}) %reduce-scatter.5.cloned.1.call-update) | async-done | bytes 1048592 | tf_op jit(solution)/shard_map/reduce_scatter | solution.py:83
  115.8 7.6 %all_gather.11 = bf16[256,1024]{1,0:T(8,128)(2,1)S(1)} all-gather(bf16[256,512]{1,0:T(8,128)(2,1)S(1)} %fusion.9), channel_id=1, replica_groups=mesh['dp'=4,'expert'=16,'tensor'=2] {'tensor'}, dimensions={1}, use_global_device_ids=true | all-gather | bytes 786432 | tf_op jit(solution)/shard_map/all_gather | solution.py:87
  123.4 4.6 %fusion.2 = bf16[256,3072]{1,0:T(8,128)(2,1)S(1)} fusion(bf16[256,1024]{1,0:T(8,128)(2,1)S(1)} %all_gather.11, bf16[1,1024,3072]{2,1,0:T(8,128)(2,1)} %param.15), kind=kOutput, calls=%fused_computation.13 | convolution fusion | flops 1611399168 | bytes 8388608 | tf_op jit(solution)/shard_map/dot_general | solution.py:94
  129.4 11.5 %all-to-all-start.2 = ((bf16[64,4,3072]{2,1,0:T(4,128)(2,1)}), bf16[64,4,3072]{2,1,0:T(4,128)(2,1)S(1)}, u32[]{:S(2)}, u32[]{:S(2)}) async-start(bf16[64,4,3072]{2,1,0:T(4,128)(2,1)} %reshape.118), calls=%async_computation.4 | async-start | bytes 3145728 | tf_op jit(solution)/shard_map/all_to_all | solution.py:46
  142.5 18.5 %all_gather.10 = bf16[512,256]{1,0:T(8,128)(2,1)S(1)} all-gather(bf16[512,128]{1,0:T(8,128)(2,1)S(1)} %fusion.11), channel_id=1, replica_groups=mesh['dp'=4,'expert'=16,'tensor'=2] {'tensor'}, dimensions={1}, use_global_device_ids=true | all-gather | bytes 393216 | tf_op jit(solution)/shard_map/all_gather | solution.py:86
  161.0 2.7 %convolution_convert_fusion = bf16[512,3072]{1,0:T(8,128)(2,1)} fusion(bf16[512,256]{1,0:T(8,128)(2,1)S(1)} %all_gather.10, bf16[256,3072]{1,0:T(8,128)(2,1)S(1)} %copy-done), kind=kOutput, calls=%fused_computation.12 | convolution fusion | flops 806879232 | bytes 4980736 | tf_op jit(solution)/shard_map/dot_general | solution.py:90
  163.7 3.1 %all-to-all-done.2 = bf16[64,4,3072]{2,1,0:T(4,128)(2,1)S(1)} async-done(((bf16[64,4,3072]{2,1,0:T(4,128)(2,1)}), bf16[64,4,3072]{2,1,0:T(4,128)(2,1)S(1)}, u32[]{:S(2)}, u32[]{:S(2)}) %all-to-all-start.2) | async-done | bytes 1572896 | tf_op jit(solution)/shard_map/all_to_all | solution.py:46
  167.9 4.9 %all-to-all-start = ((bf16[4,128,3072]{2,1,0:T(8,128)(2,1)}), bf16[4,128,3072]{2,1,0:T(8,128)(2,1)}, u32[]{:S(2)}, u32[]{:S(2)}) async-start(bf16[4,128,3072]{2,1,0:T(8,128)(2,1)} %bitcast.64), calls=%async_computation.1 | async-start | bytes 6291456 | tf_op jit(solution)/shard_map/all_to_all | solution.py:18
  173.3 2.7 %reshape.119 = bf16[256,3072]{1,0:T(8,128)(2,1)S(1)} reshape(bf16[64,4,3072]{2,1,0:T(4,128)(2,1)} %copy-done.2) | data formatting | bytes 3145728 | tf_op jit(solution)/shard_map/reshape | solution.py:98
  179.9 2.0 gather_fusion.4
  191.6 18.4 %all-to-all-done = bf16[4,128,3072]{2,1,0:T(8,128)(2,1)} async-done(((bf16[4,128,3072]{2,1,0:T(8,128)(2,1)}), bf16[4,128,3072]{2,1,0:T(8,128)(2,1)}, u32[]{:S(2)}, u32[]{:S(2)}) %all-to-all-start) | async-done | bytes 3145760 | tf_op jit(solution)/shard_map/all_to_all | solution.py:18
  210.0 2.8 %convert_reduce_fusion = f32[128,3072]{1,0:T(8,128)S(1)} fusion(bf16[4,128,3072]{2,1,0:T(8,128)(2,1)} %all-to-all-done), kind=kLoop, calls=%fused_computation.11 | loop fusion | flops 2752512 | bytes 4718592 | tf_op jit(solution)/shard_map/reduce_sum | solution.py:19
  212.8 5.9 %add_convert_fusion = bf16[128,3072]{1,0:T(8,128)(2,1)} fusion(f32[128,3072]{1,0:T(8,128)S(1)} %convert_reduce_fusion, bf16[128,3072]{1,0:T(8,128)(2,1)} %gather_fusion.8, bf16[128,3072]{1,0:T(8,128)(2,1)S(1)} %copy-done.8, bf16[128,3072]{1,0:T(8,128)(2,1)S(1)} %copy-done.7, bf16[128,3072]{1,0:T(8,128)(2,1)S(1)} %copy-done.6, ...), kind=kLoop, calls=%fused_computation.16 | loop fusion | flops 16121856 | bytes 8656896 | tf_op jit(solution)/shard_map/convert_element_type | solution.py:107
  (80 shorter events, 26.3 us)
Async XLA Ops:
  7.4 153.6 %copy-start = (bf16[256,3072]{1,0:T(8,128)(2,1)S(1)}, bf16[256,3072]{1,0:T(8,128)(2,1)}, u32[]{:S(2)}) copy-start(bf16[256,3072]{1,0:T(8,128)(2,1)} %param.17) | copy-start | bytes 4718596
  7.4 9.9 %copy-start.1 = (bf16[128,3072]{1,0:T(8,128)(2,1)S(1)}, bf16[128,3072]{1,0:T(8,128)(2,1)}, u32[]{:S(2)}) copy-start(bf16[128,3072]{1,0:T(8,128)(2,1)} %param.10) | copy-start | bytes 2359300
  7.4 80.6 %all-gather.2.cloned.1.call-start = ((), (), s32[]{:S(2)}) async-start(), calls=%async_computation.5 | async-start | bytes 3932160 | tf_op jit(solution)/shard_map/all_gather | solution.py:70
  25.4 42.5 %all-to-all-start.1 = ((bf16[64,4,3072]{2,1,0:T(4,128)(2,1)}), bf16[64,4,3072]{2,1,0:T(4,128)(2,1)S(1)}, u32[]{:S(2)}, u32[]{:S(2)}) async-start(bf16[64,4,3072]{2,1,0:T(4,128)(2,1)} %select_select_fusion), calls=%async_computation.2 | async-start | bytes 3145728 | tf_op jit(solution)/shard_map/all_to_all | solution.py:42
  37.9 76.5 %reduce-scatter.5.cloned.1.call-start = ((), (), s32[]{:S(2)}) async-start(), calls=%async_computation.7 | async-start | bytes 3145728 | tf_op jit(solution)/shard_map/reduce_scatter | solution.py:83
  79.1 62.3 %reduce-scatter.3.cloned.1.call-start = ((), (), s32[]{:S(2)}) async-start(), calls=%async_computation.6 | async-start | bytes 1572864 | tf_op jit(solution)/shard_map/reduce_scatter | solution.py:82
  129.4 37.3 %all-to-all-start.2 = ((bf16[64,4,3072]{2,1,0:T(4,128)(2,1)}), bf16[64,4,3072]{2,1,0:T(4,128)(2,1)S(1)}, u32[]{:S(2)}, u32[]{:S(2)}) async-start(bf16[64,4,3072]{2,1,0:T(4,128)(2,1)} %reshape.118), calls=%async_computation.4 | async-start | bytes 3145728 | tf_op jit(solution)/shard_map/all_to_all | solution.py:46
  166.7 1.1 copy-start.2
  166.7 6.5 %copy-start.9 = (s32[128,8]{0,1:T(8,128)S(1)}, s32[128,8]{0,1:T(8,128)}, u32[]{:S(2)}) copy-start(s32[128,8]{0,1:T(8,128)} %param.12) | copy-start | bytes 12292
  167.9 42.1 %all-to-all-start = ((bf16[4,128,3072]{2,1,0:T(8,128)(2,1)}), bf16[4,128,3072]{2,1,0:T(8,128)(2,1)}, u32[]{:S(2)}, u32[]{:S(2)}) async-start(bf16[4,128,3072]{2,1,0:T(8,128)(2,1)} %bitcast.64), calls=%async_computation.1 | async-start | bytes 6291456 | tf_op jit(solution)/shard_map/all_to_all | solution.py:18
  191.6 21.2 %copy-start.3 = (bf16[128,3072]{1,0:T(8,128)(2,1)S(1)}, bf16[128,3072]{1,0:T(8,128)(2,1)}, u32[]{:S(2)}) copy-start(bf16[128,3072]{1,0:T(8,128)(2,1)} %gather_fusion.2) | copy-start | bytes 2359300
  191.6 21.2 %copy-start.4 = (bf16[128,3072]{1,0:T(8,128)(2,1)S(1)}, bf16[128,3072]{1,0:T(8,128)(2,1)}, u32[]{:S(2)}) copy-start(bf16[128,3072]{1,0:T(8,128)(2,1)} %gather_fusion.3) | copy-start | bytes 2359300
  210.0 2.8 %copy-start.5 = (bf16[128,3072]{1,0:T(8,128)(2,1)S(1)}, bf16[128,3072]{1,0:T(8,128)(2,1)}, u32[]{:S(2)}) copy-start(bf16[128,3072]{1,0:T(8,128)(2,1)} %gather_fusion.4) | copy-start | bytes 2359300
  210.0 2.8 %copy-start.6 = (bf16[128,3072]{1,0:T(8,128)(2,1)S(1)}, bf16[128,3072]{1,0:T(8,128)(2,1)}, u32[]{:S(2)}) copy-start(bf16[128,3072]{1,0:T(8,128)(2,1)} %gather_fusion.5) | copy-start | bytes 2359300
  210.0 2.8 %copy-start.7 = (bf16[128,3072]{1,0:T(8,128)(2,1)S(1)}, bf16[128,3072]{1,0:T(8,128)(2,1)}, u32[]{:S(2)}) copy-start(bf16[128,3072]{1,0:T(8,128)(2,1)} %gather_fusion.6) | copy-start | bytes 2359300
  210.0 2.9 %copy-start.8 = (bf16[128,3072]{1,0:T(8,128)(2,1)S(1)}, bf16[128,3072]{1,0:T(8,128)(2,1)}, u32[]{:S(2)}) copy-start(bf16[128,3072]{1,0:T(8,128)(2,1)} %gather_fusion.7) | copy-start | bytes 2359300
Sparse Core Ops, SparseCore 0:
  9.8 59.5 all-gather.1
Sparse Core Ops, SparseCore 1:
  79.2 35.1 reduce-scatter.4
  116.6 23.8 reduce-scatter.2
where the time goes:
time: 227 us; the launch traced here: 226 us
  local copies, waits for them, and re-layouts  67.8 us (30%)
  waiting for transfers between devices  42.2 us (19%)
  starting transfers between devices  29.1 us (13%)
  blocking collectives  26.1 us (11%)
  matrix products  23.7 us (10%)
  other arithmetic  22 us (10%)
  between operations  15.2 us (7%)
    reduce_scatter x1, waiting for transfers between devices, shards(): lax.psum_scatter(routed_partial, 'tensor', scatter_dimension=2, tiled=True)  20 us
    unnamed x23, local copies, waits for them, and re-layouts  19.2 us
    all_gather x1, blocking collectives, shards(): lax.all_gather(swiglu(shared_half), 'tensor', axis=1, tiled=True)  18.5 us
    all_to_all x1, waiting for transfers between devices, summed_on_arrival(): lax.all_to_all(parts, axis, split_axis=0, concat_axis=0, tiled=True)  18.4 us
    dot_general x1, local copies, waits for them, and re-layouts, shards(): jnp.dot(rows, expert_in[0].reshape(half_width, -1), preferred_element_typ...  16.6 us
    gather x8, local copies, waits for them, and re-layouts, shards(): jnp.take(returned, jnp.maximum(index, 0), axis=0).astype(jnp.float32)  15.5 us
    all_to_all x1, starting transfers between devices, dispatch_rows(): lax.all_to_all(send_rows, ('dp', 'expert'), split_axis=0, concat_axis=0,...  12.5 us
    all_to_all x1, starting transfers between devices, return_rows(): lax.all_to_all(answers, ('dp', 'expert'), split_axis=0, concat_axis=0, ti...  11.5 us
  transfers between devices with their start and end apart: 6, of which 3 were waited for; matrix products, arithmetic and copies ran while one was open for 46% of the time, Pallas kernels for 0%

commit v1 on v0

--- a/solution.py
+++ b/solution.py
@@ -6,6 +6,11 @@
 EXPERTS = 384
 CAP = 4
 gate_scale = 1.0 / 65536.0
+
+
+def swapped_in(shard, axis, dim):
+    sent = jnp.stack([shard] * lax.axis_size(axis))
+    return jnp.concatenate(lax.all_to_all(sent, axis, 0, 0), axis=dim)
 
 
 def in_blocks(array, dim, devices):
@@ -83,7 +88,7 @@
         lax.psum_scatter(routed_partial, "tensor", scatter_dimension=2, tiled=True),
     )
     shared_act, routed_act = (
-        lax.all_gather(swiglu(shared_half), "tensor", axis=1, tiled=True),
+        swapped_in(swiglu(shared_half), "tensor", 1),
         lax.all_gather(swiglu(routed_half), "tensor", axis=1, tiled=True),
     )
     shared_part = summed_on_arrival(

time: 227 us -> 249 us (1.097)
  waiting for transfers between devices: 42.2 us -> 76.3 us
  blocking collectives: 26.1 us -> 7.73 us
    all_gather x1 -> x0, blocking collectives: 18.5 us -> none  [shards(): lax.all_gather(swiglu(shared_half), 'tensor', axis=1, tiled=True)]
    all_to_all x1, waiting for transfers between devices: 3.06 us -> 20.3 us  [return_rows(): lax.all_to_all(answers, ('dp', 'expert'), split_axis=0, concat_axis=0, ti...]
    reduce_scatter x1, waiting for transfers between devices: 0.03 us -> 17 us  [shards(): lax.psum_scatter(shared_partial, 'tensor', scatter_dimension=2, tiled=True)]
    all_to_all x0 -> x1, starting transfers between devices: none -> 3.44 us  [swapped_in(): return jnp.concatenate(lax.all_to_all(sent, axis, 0, 0), axis=dim)]
    unnamed x23 -> x29, local copies, waits for them, and re-layouts: 19.2 us -> 19.9 us
  transfers between devices with their start and end apart: 6 -> 7, of which waited for: 3 -> 4; matrix products, arithmetic and copies ran while one was open for 46% -> 42% of each run, Pallas kernels for 0% -> 0%
where the time goes in v1:
time: 249 us; the launch traced here: 248 us
  waiting for transfers between devices  76.3 us (31%)
  local copies, waits for them, and re-layouts  69.6 us (28%)
  starting transfers between devices  31.5 us (13%)
  matrix products  23.8 us (10%)
  other arithmetic  23.6 us (9%)
  between operations  15.3 us (6%)
  blocking collectives  7.73 us (3%)
    all_to_all x1, waiting for transfers between devices, return_rows(): lax.all_to_all(answers, ('dp', 'expert'), split_axis=0, concat_axis=0, ti...  20.3 us
    reduce_scatter x1, waiting for transfers between devices, shards(): lax.psum_scatter(routed_partial, 'tensor', scatter_dimension=2, tiled=True)  20.1 us
    unnamed x29, local copies, waits for them, and re-layouts  19.9 us
    all_to_all x1, waiting for transfers between devices, summed_on_arrival(): lax.all_to_all(parts, axis, split_axis=0, concat_axis=0, tiled=True)  18.1 us
    reduce_scatter x1, waiting for transfers between devices, shards(): lax.psum_scatter(shared_partial, 'tensor', scatter_dimension=2, tiled=True)  17 us
    dot_general x1, local copies, waits for them, and re-layouts, shards(): jnp.dot(rows, expert_in[0].reshape(half_width, -1), preferred_element_typ...  16.6 us
    gather x8, local copies, waits for them, and re-layouts, shards(): jnp.take(returned, jnp.maximum(index, 0), axis=0).astype(jnp.float32)  15.5 us
    all_to_all x1, starting transfers between devices, dispatch_rows(): lax.all_to_all(send_rows, ('dp', 'expert'), split_axis=0, concat_axis=0,...  12.5 us
  transfers between devices with their start and end apart: 7, of which 4 were waited for; matrix products, arithmetic and copies ran while one was open for 42% of the time, Pallas kernels for 0%

profile of v1, /device:TPU:1, one launch (start us, length us, event | category | flops | bytes accessed | tf_op | source)
XLA Modules:
  0.0 247.9 jit_solution(6258748380258505941)
XLA Ops:
  10.4 4.8 %select_reduce_fusion = (s32[128,8]{1,0:T(8,128)S(1)}, s32[128,8]{1,0:T(8,128)S(1)}) fusion(s32[384]{0:T(512)S(1)} %select_reduce_fusion.4, s32[128,8]{1,0:T(8,128)S(1)} %copy.25, s32[384]{0:T(512)S(1)} %select_reduce_fusion.5), kind=kLoop, calls=%fused_computation.18 | loop fusion | flops 1964032 | bytes 15360 | tf_op jit(solution)/shard_map/reduce_sum | solution.py:38
  17.4 2.7 %gather_fusion = bf16[256,3072]{1,0:T(8,128)(2,1)} fusion(bf16[128,3072]{1,0:T(8,128)(2,1)S(1)} %copy-done.1, s32[1024]{0:T(1024)S(1)} %pad_clamp_fusion.8), kind=kCustom, calls=%fused_computation.8 | custom fusion | bytes 3146752 | tf_op jit(solution)/shard_map/jit(_take)/gather | solution.py:73
  20.1 2.9 %gather.10 = bf16[64,4,3072]{2,1,0:T(4,128)(2,1)S(1)} reshape(bf16[256,3072]{1,0:T(8,128)(2,1)} %gather_fusion) | data formatting | bytes 3145728 | tf_op jit(solution)/shard_map/jit(_take)/gather | solution.py:73
  23.0 2.4 select_select_fusion
  25.4 12.5 %all-to-all-start.2 = ((bf16[64,4,3072]{2,1,0:T(4,128)(2,1)}), bf16[64,4,3072]{2,1,0:T(4,128)(2,1)S(1)}, u32[]{:S(2)}, u32[]{:S(2)}) async-start(bf16[64,4,3072]{2,1,0:T(4,128)(2,1)} %select_select_fusion), calls=%async_computation.3 | async-start | bytes 3145728 | tf_op jit(solution)/shard_map/all_to_all | solution.py:47
  38.2 13.1 %copy.28 = bf16[384,8,2,1024]{3,1,2,0:T(8,128)(2,1)} copy(bf16[384,8,2,1024]{3,2,1,0:T(2,128)(2,1)} %bitcast.67) | data formatting | bytes 25165824
  51.3 16.6 %copy.26 = bf16[2048,3072]{1,0:T(8,128)(2,1)} copy(bf16[2048,3072]{0,1:T(8,128)(2,1)} %bitcast.65) | data formatting | bytes 25165824 | tf_op jit(solution)/shard_map/dot_general | solution.py:82
  69.3 9.9 %fusion.18 = f32[256,2,1024]{2,0,1:T(8,128)} fusion(bf16[256,3072,1]{1,0,2:T(8,128)(2,1)} %reshape.267, bf16[2,1024,3072]{2,1,0:T(8,128)(2,1)} %bitcast.68), kind=kOutput, calls=%fused_computation.102 | convolution fusion | flops 3221225472 | bytes 16252928 | tf_op jit(solution)/shard_map/dot_general | solution.py:82
  79.2 4.1 %copy.27 = bf16[384,8,2,256]{3,1,2,0:T(8,128)(2,1)} copy(bf16[384,8,2,256]{3,2,1,0:T(2,128)(2,1)} %bitcast.70) | data formatting | bytes 6291456
  83.3 4.6 %copy.23 = bf16[512,3072]{1,0:T(8,128)(2,1)} copy(bf16[512,3072]{0,1:T(8,128)(2,1)} %bitcast.69) | data formatting | bytes 6291456 | tf_op jit(solution)/shard_map/dot_general | solution.py:76
  88.0 6.3 %fusion.5 = f32[512,2,256]{2,0,1:T(8,128)} fusion(bf16[2,256,3072]{2,1,0:T(8,128)(2,1)} %bitcast.71, bf16[512,3072]{1,0:T(8,128)(2,1)} %all-gather.2.cloned.1.call-done), kind=kOutput, calls=%fused_computation.14 | convolution fusion | flops 1610612736 | bytes 7340032 | tf_op jit(solution)/shard_map/dot_general | solution.py:76
  94.3 20.1 %reduce-scatter.5.cloned.1.call-done = f32[256,2,512]{2,0,1:T(8,128)} async-done(((f32[256,2,1024]{2,0,1:T(8,128)}), f32[256,2,512]{2,0,1:T(8,128)}) %reduce-scatter.5.cloned.1.call-update) | async-done | bytes 1048592 | tf_op jit(solution)/shard_map/reduce_scatter | solution.py:88
  115.8 7.7 %all_gather.7 = bf16[256,1024]{1,0:T(8,128)(2,1)} all-gather(bf16[256,512]{1,0:T(8,128)(2,1)S(1)} %fusion.9), channel_id=1, replica_groups=mesh['dp'=4,'expert'=16,'tensor'=2] {'tensor'}, dimensions={1}, use_global_device_ids=true | all-gather | bytes 786432 | tf_op jit(solution)/shard_map/all_gather | solution.py:92
  123.5 17.0 %reduce-scatter.3.cloned.1.call-done = f32[512,2,128]{2,0,1:T(8,128)} async-done(((f32[512,2,256]{2,0,1:T(8,128)}), f32[512,2,128]{2,0,1:T(8,128)}) %reduce-scatter.3.cloned.1.call-update) | async-done | bytes 524304 | tf_op jit(solution)/shard_map/reduce_scatter | solution.py:87
  142.3 3.4 %all-to-all-start = ((bf16[2,512,128]{2,1,0:T(8,128)(2,1)}), bf16[2,512,128]{2,1,0:T(8,128)(2,1)S(1)}, u32[]{:S(2)}, u32[]{:S(2)}) async-start(bf16[2,512,128]{2,1,0:T(8,128)(2,1)} %pad_maximum_fusion), calls=%async_computation.1 | async-start | bytes 524288 | tf_op jit(solution)/shard_map/all_to_all | solution.py:13
  145.8 4.8 %fusion.2 = bf16[256,3072]{1,0:T(8,128)(2,1)S(1)} fusion(bf16[256,1024]{1,0:T(8,128)(2,1)} %all_gather.7, bf16[1,1024,3072]{2,1,0:T(8,128)(2,1)} %param.15), kind=kOutput, calls=%fused_computation.13 | convolution fusion | flops 1611399168 | bytes 8388608 | tf_op jit(solution)/shard_map/dot_general | solution.py:99
  152.8 10.5 %all-to-all-start.3 = ((bf16[64,4,3072]{2,1,0:T(4,128)(2,1)}), bf16[64,4,3072]{2,1,0:T(4,128)(2,1)S(1)}, u32[]{:S(2)}, u32[]{:S(2)}) async-start(bf16[64,4,3072]{2,1,0:T(4,128)(2,1)} %reshape.167), calls=%async_computation.5 | async-start | bytes 3145728 | tf_op jit(solution)/shard_map/all_to_all | solution.py:51
  165.7 2.7 %convolution_convert_fusion = bf16[512,3072]{1,0:T(8,128)(2,1)} fusion(bf16[512,256]{0,1:T(8,128)(2,1)S(1)} %bitcast.72, bf16[256,3072]{1,0:T(8,128)(2,1)S(1)} %copy-done), kind=kOutput, calls=%fused_computation.12 | convolution fusion | flops 806879232 | bytes 4980736 | tf_op jit(solution)/shard_map/dot_general | solution.py:95
  168.3 20.3 %all-to-all-done.3 = bf16[64,4,3072]{2,1,0:T(4,128)(2,1)S(1)} async-done(((bf16[64,4,3072]{2,1,0:T(4,128)(2,1)}), bf16[64,4,3072]{2,1,0:T(4,128)(2,1)S(1)}, u32[]{:S(2)}, u32[]{:S(2)}) %all-to-all-start.3) | async-done | bytes 1572896 | tf_op jit(solution)/shard_map/all_to_all | solution.py:51
  189.8 4.9 %all-to-all-start.1 = ((bf16[4,128,3072]{2,1,0:T(8,128)(2,1)}), bf16[4,128,3072]{2,1,0:T(8,128)(2,1)}, u32[]{:S(2)}, u32[]{:S(2)}) async-start(bf16[4,128,3072]{2,1,0:T(8,128)(2,1)} %bitcast.66), calls=%async_computation.2 | async-start | bytes 6291456 | tf_op jit(solution)/shard_map/all_to_all | solution.py:23
  195.3 2.7 %reshape.168 = bf16[256,3072]{1,0:T(8,128)(2,1)S(1)} reshape(bf16[64,4,3072]{2,1,0:T(4,128)(2,1)} %copy-done.2) | data formatting | bytes 3145728 | tf_op jit(solution)/shard_map/reshape | solution.py:103
  213.6 18.1 %all-to-all-done.1 = bf16[4,128,3072]{2,1,0:T(8,128)(2,1)} async-done(((bf16[4,128,3072]{2,1,0:T(8,128)(2,1)}), bf16[4,128,3072]{2,1,0:T(8,128)(2,1)}, u32[]{:S(2)}, u32[]{:S(2)}) %all-to-all-start.1) | async-done | bytes 3145760 | tf_op jit(solution)/shard_map/all_to_all | solution.py:23
  231.7 2.8 %convert_reduce_fusion = f32[128,3072]{1,0:T(8,128)S(1)} fusion(bf16[4,128,3072]{2,1,0:T(8,128)(2,1)} %all-to-all-done.1), kind=kLoop, calls=%fused_computation.11 | loop fusion | flops 2752512 | bytes 4718592 | tf_op jit(solution)/shard_map/reduce_sum | solution.py:24
  234.6 5.9 %add_convert_fusion = bf16[128,3072]{1,0:T(8,128)(2,1)} fusion(f32[128,3072]{1,0:T(8,128)S(1)} %convert_reduce_fusion, bf16[128,3072]{1,0:T(8,128)(2,1)} %gather_fusion.8, bf16[128,3072]{1,0:T(8,128)(2,1)S(1)} %copy-done.8, bf16[128,3072]{1,0:T(8,128)(2,1)S(1)} %copy-done.7, bf16[128,3072]{1,0:T(8,128)(2,1)S(1)} %copy-done.6, ...), kind=kLoop, calls=%fused_computation.16 | loop fusion | flops 16121856 | bytes 8656896 | tf_op jit(solution)/shard_map/convert_element_type | solution.py:112
  (89 shorter events, 31.7 us)
Async XLA Ops:
  7.4 158.3 %copy-start = (bf16[256,3072]{1,0:T(8,128)(2,1)S(1)}, bf16[256,3072]{1,0:T(8,128)(2,1)}, u32[]{:S(2)}) copy-start(bf16[256,3072]{1,0:T(8,128)(2,1)} %param.17) | copy-start | bytes 4718596
  7.4 10.0 %copy-start.1 = (bf16[128,3072]{1,0:T(8,128)(2,1)S(1)}, bf16[128,3072]{1,0:T(8,128)(2,1)}, u32[]{:S(2)}) copy-start(bf16[128,3072]{1,0:T(8,128)(2,1)} %param.10) | copy-start | bytes 2359300
  7.4 80.6 %all-gather.2.cloned.1.call-start = ((), (), s32[]{:S(2)}) async-start(), calls=%async_computation.6 | async-start | bytes 3932160 | tf_op jit(solution)/shard_map/all_gather | solution.py:75
  15.2 2.2 copy-start.10
  16.5 0.9 copy-start.11
  25.4 42.5 %all-to-all-start.2 = ((bf16[64,4,3072]{2,1,0:T(4,128)(2,1)}), bf16[64,4,3072]{2,1,0:T(4,128)(2,1)S(1)}, u32[]{:S(2)}, u32[]{:S(2)}) async-start(bf16[64,4,3072]{2,1,0:T(4,128)(2,1)} %select_select_fusion), calls=%async_computation.3 | async-start | bytes 3145728 | tf_op jit(solution)/shard_map/all_to_all | solution.py:47
  37.9 76.5 %reduce-scatter.5.cloned.1.call-start = ((), (), s32[]{:S(2)}) async-start(), calls=%async_computation.8 | async-start | bytes 3145728 | tf_op jit(solution)/shard_map/reduce_scatter | solution.py:88
  79.2 61.4 %reduce-scatter.3.cloned.1.call-start = ((), (), s32[]{:S(2)}) async-start(), calls=%async_computation.7 | async-start | bytes 1572864 | tf_op jit(solution)/shard_map/reduce_scatter | solution.py:87
  142.3 9.7 %all-to-all-start = ((bf16[2,512,128]{2,1,0:T(8,128)(2,1)}), bf16[2,512,128]{2,1,0:T(8,128)(2,1)S(1)}, u32[]{:S(2)}, u32[]{:S(2)}) async-start(bf16[2,512,128]{2,1,0:T(8,128)(2,1)} %pad_maximum_fusion), calls=%async_computation.1 | async-start | bytes 524288 | tf_op jit(solution)/shard_map/all_to_all | solution.py:13
  152.0 0.7 copy-start.9
  152.8 35.9 %all-to-all-start.3 = ((bf16[64,4,3072]{2,1,0:T(4,128)(2,1)}), bf16[64,4,3072]{2,1,0:T(4,128)(2,1)S(1)}, u32[]{:S(2)}, u32[]{:S(2)}) async-start(bf16[64,4,3072]{2,1,0:T(4,128)(2,1)} %reshape.167), calls=%async_computation.5 | async-start | bytes 3145728 | tf_op jit(solution)/shard_map/all_to_all | solution.py:51
  188.7 1.1 copy-start.2
  188.7 6.5 %copy-start.12 = (s32[128,8]{0,1:T(8,128)S(1)}, s32[128,8]{0,1:T(8,128)}, u32[]{:S(2)}) copy-start(s32[128,8]{0,1:T(8,128)} %param.12) | copy-start | bytes 12292
  189.8 41.9 %all-to-all-start.1 = ((bf16[4,128,3072]{2,1,0:T(8,128)(2,1)}), bf16[4,128,3072]{2,1,0:T(8,128)(2,1)}, u32[]{:S(2)}, u32[]{:S(2)}) async-start(bf16[4,128,3072]{2,1,0:T(8,128)(2,1)} %bitcast.66), calls=%async_computation.2 | async-start | bytes 6291456 | tf_op jit(solution)/shard_map/all_to_all | solution.py:23
  213.6 20.9 %copy-start.3 = (bf16[128,3072]{1,0:T(8,128)(2,1)S(1)}, bf16[128,3072]{1,0:T(8,128)(2,1)}, u32[]{:S(2)}) copy-start(bf16[128,3072]{1,0:T(8,128)(2,1)} %gather_fusion.2) | copy-start | bytes 2359300
  213.6 20.9 %copy-start.4 = (bf16[128,3072]{1,0:T(8,128)(2,1)S(1)}, bf16[128,3072]{1,0:T(8,128)(2,1)}, u32[]{:S(2)}) copy-start(bf16[128,3072]{1,0:T(8,128)(2,1)} %gather_fusion.3) | copy-start | bytes 2359300
  231.7 2.8 %copy-start.5 = (bf16[128,3072]{1,0:T(8,128)(2,1)S(1)}, bf16[128,3072]{1,0:T(8,128)(2,1)}, u32[]{:S(2)}) copy-start(bf16[128,3072]{1,0:T(8,128)(2,1)} %gather_fusion.4) | copy-start | bytes 2359300
  231.7 2.8 %copy-start.6 = (bf16[128,3072]{1,0:T(8,128)(2,1)S(1)}, bf16[128,3072]{1,0:T(8,128)(2,1)}, u32[]{:S(2)}) copy-start(bf16[128,3072]{1,0:T(8,128)(2,1)} %gather_fusion.5) | copy-start | bytes 2359300
  231.7 2.8 %copy-start.7 = (bf16[128,3072]{1,0:T(8,128)(2,1)S(1)}, bf16[128,3072]{1,0:T(8,128)(2,1)}, u32[]{:S(2)}) copy-start(bf16[128,3072]{1,0:T(8,128)(2,1)} %gather_fusion.6) | copy-start | bytes 2359300
  231.7 2.9 %copy-start.8 = (bf16[128,3072]{1,0:T(8,128)(2,1)S(1)}, bf16[128,3072]{1,0:T(8,128)(2,1)}, u32[]{:S(2)}) copy-start(bf16[128,3072]{1,0:T(8,128)(2,1)} %gather_fusion.7) | copy-start | bytes 2359300
Sparse Core Ops, SparseCore 0:
  9.8 59.5 all-gather.1
Sparse Core Ops, SparseCore 1:
  79.2 35.2 reduce-scatter.4
  116.7 23.8 reduce-scatter.2
